TPU v7x, 32 devices: a whole 2x2x4 slice. The times are simulated.
32 devices in a mesh: seq: 4 (over z), fsdp: 8 (over y, x, core).
Axes of the slice: x: 2, y: 2, z: 4, core: 2. Of those that a mesh axis runs over, the one named last changes fastest.
Arguments:
- tokens: float32 [16, 1024, 1536], P('fsdp', 'seq'), may hold values from -6 to 6
- cotangent: float32 [16, 1024, 1536], P('fsdp', 'seq'), may hold values from -6 to 6
- attention_gain: bfloat16 [1536], P('fsdp'), may hold values from 0.5 to 1.5
- feedforward_gain: bfloat16 [1536], P('fsdp'), may hold values from 0.5 to 1.5
- query_weight: bfloat16 [1536, 1536], P('fsdp'), may hold values from -1 to 1
- key_matrix: bfloat16 [1536, 768], P('fsdp'), may hold values from -16 to 16
- value_matrix: bfloat16 [1536, 768], P('fsdp'), may hold values from -0.15625 to 0.15625
- out_weight: bfloat16 [1536, 1536], P('fsdp'), may hold values from -1.25 to 1.25
- gate_weight: bfloat16 [1536, 4096], P('fsdp'), may hold values from -0.15625 to 0.15625
- up_weight: bfloat16 [1536, 4096], P('fsdp'), may hold values from -0.15625 to 0.15625
- down_weight: bfloat16 [4096, 1536], P('fsdp'), may hold values from -0.09375 to 0.09375
Outputs:
- block_out: float32 [16, 1024, 1536], P('fsdp', 'seq')
- grad_tokens: float32 [16, 1024, 1536], P('fsdp', 'seq')
- grad_attention_gain: float32 [1536], P('fsdp')
- grad_feedforward_gain: float32 [1536], P('fsdp')
- grad_query: float32 [1536, 1536], P('fsdp')
- grad_key: float32 [1536, 768], P('fsdp')
- grad_value: float32 [1536, 768], P('fsdp')
- grad_out: float32 [1536, 1536], P('fsdp')
- grad_gate: float32 [1536, 4096], P('fsdp')
- grad_up: float32 [1536, 4096], P('fsdp')
- grad_down: float32 [4096, 1536], P('fsdp')
All inputs are finite; a program needn't handle non-finite values.
Results may differ from a plain program's by a relative error of at most 0.024.
The roundings to bfloat16 on the way count: a program that leaves them out, or rounds other values in their place, can miss the bound.
Values may be sent and summed in bfloat16 or wider, within the bound.
A program may use at most 320 MiB of HBM per device.

v0:
```python
from functools import partial
import math
import jax
import jax.numpy as jnp
from jax import lax
from jax.sharding import PartitionSpec as P

QUERY_HEADS = 16
KEY_VALUE_HEADS = 8
HEAD_DIM = 96
norm_eps = 1e-05
rope_base = 100000.0
masked_score = -1e30


def rope_tables(positions, head_size):
    half = head_size // 2
    freqs = rope_base ** (-(2.0 * jnp.arange(half, dtype=jnp.float32)) / head_size)
    angles = positions.astype(jnp.float32)[:, None] * freqs[None, :]
    return (jnp.cos(angles), jnp.sin(angles))


def rotate_halves(values, cosine, sine):
    half = values.shape[-1] // 2
    first = values[..., :half]
    second = values[..., half:]
    return jnp.concatenate(
        [first * cosine - second * sine, second * cosine + first * sine], axis=-1
    )


def reverse_rotation(grads, cosine, sine):
    half = grads.shape[-1] // 2
    first = grads[..., :half]
    second = grads[..., half:]
    return jnp.concatenate(
        [first * cosine + second * sine, second * cosine - first * sine], axis=-1
    )


def masked_scores(query_rows, key_rows, scale):
    sequence_length = query_rows.shape[0]
    scores = (
        jnp.einsum("qhgd,khd->hgqk", query_rows, key_rows, preferred_element_type=jnp.float32)
        * scale
    )
    causal = jnp.arange(sequence_length)[:, None] >= jnp.arange(sequence_length)[None, :]
    return jnp.where(causal, scores, masked_score)


def attend_items(packed_arrays, group_size, head_size):
    count, sequence_length, features = packed_arrays.shape
    kv_local = features // ((group_size + 2) * head_size)
    scale = 1.0 / math.sqrt(head_size)

    def single(item):
        split = item.reshape(sequence_length, kv_local, group_size + 2, head_size)
        query_rows = split[:, :, :group_size, :]
        key_rows = split[:, :, group_size, :]
        value_matrix_rows = split[:, :, group_size + 1, :]
        scores = masked_scores(query_rows, key_rows, scale)
        top_score = jnp.max(scores, axis=-1, keepdims=True)
        log_total = top_score + jnp.log(
            jnp.sum(jnp.exp(scores - top_score), axis=-1, keepdims=True)
        )
        probs = jnp.exp(scores - log_total).astype(jnp.bfloat16)
        attended = jnp.einsum(
            "hgqk,khd->qhgd", probs, value_matrix_rows, preferred_element_type=jnp.float32
        )
        return (
            attended.astype(jnp.bfloat16).reshape(
                sequence_length, kv_local * group_size * head_size
            ),
            log_total[..., 0],
        )

    attended_all, log_totals = lax.map(single, packed_arrays)
    return (attended_all, log_totals, packed_arrays)


def attend_back_item(inputs, group_size, head_size, cosine, sine):
    packed_item, attended_item, log_total, grad_item = inputs
    sequence_length = packed_item.shape[0]
    kv_local = packed_item.shape[1] // ((group_size + 2) * head_size)
    scale = 1.0 / math.sqrt(head_size)
    split = packed_item.reshape(sequence_length, kv_local, group_size + 2, head_size)
    query_rows = split[:, :, :group_size, :]
    key_rows = split[:, :, group_size, :]
    value_matrix_rows = split[:, :, group_size + 1, :]
    out_heads = attended_item.reshape(sequence_length, kv_local, group_size, head_size)
    grad_heads = grad_item.reshape(sequence_length, kv_local, group_size, head_size)
    scores = masked_scores(query_rows, key_rows, scale)
    probs = jnp.exp(scores - log_total[..., None])
    delta = jnp.einsum("qhgd,qhgd->hgq", grad_heads, out_heads, preferred_element_type=jnp.float32)
    value_gradients = jnp.einsum(
        "hgqk,qhgd->khd", probs.astype(jnp.bfloat16), grad_heads, preferred_element_type=jnp.float32
    )
    grad_probs = jnp.einsum(
        "qhgd,khd->hgqk", grad_heads, value_matrix_rows, preferred_element_type=jnp.float32
    )
    grad_scores = (probs * (grad_probs - delta[..., None]) * scale).astype(jnp.bfloat16)
    grad_queries = jnp.einsum(
        "hgqk,khd->qhgd", grad_scores, key_rows, preferred_element_type=jnp.float32
    )
    key_gradients = jnp.einsum(
        "hgqk,qhgd->khd", grad_scores, query_rows, preferred_element_type=jnp.float32
    )
    grad_queries = reverse_rotation(grad_queries, cosine[:, None, None, :], sine[:, None, None, :])
    key_gradients = reverse_rotation(key_gradients, cosine[:, None, :], sine[:, None, :])
    stacked = jnp.concatenate(
        [
            grad_queries.astype(jnp.bfloat16),
            key_gradients.astype(jnp.bfloat16)[:, :, None, :],
            value_gradients.astype(jnp.bfloat16)[:, :, None, :],
        ],
        axis=2,
    )
    return stacked.reshape(sequence_length, kv_local * (group_size + 2) * head_size)


def norm_back(grad_normed, normed, inverse, gain):
    scaled = grad_normed * gain
    return inverse * (scaled - normed * jnp.mean(scaled * normed, axis=-1, keepdims=True))


def body(
    tokens,
    cotangent,
    attention_gain,
    feedforward_gain,
    query_weight,
    key_matrix,
    value_matrix,
    out_weight,
    gate_weight,
    up_weight,
    down_weight,
):
    sequence_count, span_length, width = tokens.shape
    row_count = sequence_count * span_length
    group_size = QUERY_HEADS // KEY_VALUE_HEADS
    gain_low_one, gain_low_two, whole_query, whole_key, whole_value, whole_out = (
        lax.all_gather(attention_gain, "fsdp", axis=0, tiled=True),
        lax.all_gather(feedforward_gain, "fsdp", axis=0, tiled=True),
        lax.all_gather(query_weight, "fsdp", axis=0, tiled=True),
        lax.all_gather(key_matrix, "fsdp", axis=0, tiled=True),
        lax.all_gather(value_matrix, "fsdp", axis=0, tiled=True),
        lax.all_gather(out_weight, "fsdp", axis=0, tiled=True),
    )
    gain_one = gain_low_one.astype(jnp.float32)
    gain_two = gain_low_two.astype(jnp.float32)
    positions = lax.axis_index("seq") * span_length + jnp.arange(span_length, dtype=jnp.int32)
    cosine, sine = rope_tables(positions, HEAD_DIM)
    cosine_rows = jnp.tile(cosine, (sequence_count, 1))[:, None, :]
    sine_rows = jnp.tile(sine, (sequence_count, 1))[:, None, :]
    flat = tokens.reshape(row_count, width)
    inv_one = lax.rsqrt(jnp.mean(flat * flat, axis=-1, keepdims=True) + norm_eps)
    normed_one = flat * inv_one
    first_inputs = (normed_one * gain_one).astype(jnp.bfloat16)
    query_projected = jnp.dot(
        first_inputs, whole_query, preferred_element_type=jnp.float32
    ).reshape(row_count, QUERY_HEADS, HEAD_DIM)
    key_projected = jnp.dot(first_inputs, whole_key, preferred_element_type=jnp.float32).reshape(
        row_count, KEY_VALUE_HEADS, HEAD_DIM
    )
    value_matrix_rows = jnp.dot(
        first_inputs, whole_value, preferred_element_type=jnp.float32
    ).astype(jnp.bfloat16)
    query_rotated = (
        rotate_halves(query_projected, cosine_rows, sine_rows)
        .astype(jnp.bfloat16)
        .reshape(row_count, KEY_VALUE_HEADS, group_size, HEAD_DIM)
    )
    key_rotated = (
        rotate_halves(key_projected, cosine_rows, sine_rows)
        .astype(jnp.bfloat16)
        .reshape(row_count, KEY_VALUE_HEADS, 1, HEAD_DIM)
    )
    packed_arrays = jnp.concatenate(
        [
            query_rotated,
            key_rotated,
            value_matrix_rows.reshape(row_count, KEY_VALUE_HEADS, 1, HEAD_DIM),
        ],
        axis=2,
    )
    packed_arrays = packed_arrays.reshape(
        sequence_count, span_length, KEY_VALUE_HEADS * (group_size + 2) * HEAD_DIM
    )
    attend_fn = partial(attend_items, group_size=group_size, head_size=HEAD_DIM)
    heads_attended, log_totals, head_inputs = attend_fn(
        lax.all_to_all(packed_arrays, "seq", split_axis=2, concat_axis=1, tiled=True)
    )
    attended_flat = lax.all_to_all(
        heads_attended, "seq", split_axis=1, concat_axis=2, tiled=True
    ).reshape(row_count, QUERY_HEADS * HEAD_DIM)
    hidden_one = flat + jnp.dot(attended_flat, whole_out, preferred_element_type=jnp.float32)
    inv_two = lax.rsqrt(jnp.mean(hidden_one * hidden_one, axis=-1, keepdims=True) + norm_eps)
    normed_two = hidden_one * inv_two
    inputs_two = (normed_two * gain_two).astype(jnp.bfloat16)
    pieces = (
        lax.all_gather(gate_weight, "fsdp", axis=0, tiled=True),
        lax.all_gather(up_weight, "fsdp", axis=0, tiled=True),
    )
    columns = inputs_two
    gate_pre = jnp.dot(columns, pieces[0], preferred_element_type=jnp.float32)
    up_pre = jnp.dot(columns, pieces[1], preferred_element_type=jnp.float32)
    sigmoid_gate = jax.nn.sigmoid(gate_pre)
    hidden_act = (gate_pre * sigmoid_gate * up_pre).astype(jnp.bfloat16)
    columns = hidden_act
    ffn_result = jnp.dot(
        columns,
        lax.all_gather(down_weight, "fsdp", axis=0, tiled=True),
        preferred_element_type=jnp.float32,
    )
    block_out = hidden_one + ffn_result
    grad_flat = cotangent.reshape(row_count, width)
    grad_low = grad_flat.astype(jnp.bfloat16)
    grad_down = jnp.dot(hidden_act.T, grad_low, preferred_element_type=jnp.float32)
    grad_hidden = jnp.dot(
        grad_low,
        lax.all_gather(down_weight, "fsdp", axis=0, tiled=True).T,
        preferred_element_type=jnp.float32,
    )
    grad_gate_pre = (
        grad_hidden * up_pre * sigmoid_gate * (1.0 + gate_pre * (1.0 - sigmoid_gate))
    ).astype(jnp.bfloat16)
    grad_up_pre = (grad_hidden * gate_pre * sigmoid_gate).astype(jnp.bfloat16)
    grad_gate = jnp.dot(inputs_two.T, grad_gate_pre, preferred_element_type=jnp.float32)
    grad_up = jnp.dot(inputs_two.T, grad_up_pre, preferred_element_type=jnp.float32)
    pieces = (
        lax.all_gather(gate_weight, "fsdp", axis=0, tiled=True),
        lax.all_gather(up_weight, "fsdp", axis=0, tiled=True),
    )
    block = jnp.dot(grad_gate_pre, pieces[0].T, preferred_element_type=jnp.float32) + jnp.dot(
        grad_up_pre, pieces[1].T, preferred_element_type=jnp.float32
    )
    gain_grad_two = jnp.sum(block * normed_two, axis=0)
    grad_hidden_one = grad_flat + norm_back(block, normed_two, inv_two, gain_two)
    ffn_shards = (
        lax.psum_scatter(
            gain_grad_two.astype(jnp.bfloat16), "fsdp", scatter_dimension=0, tiled=True
        ).astype(jnp.float32),
        lax.psum_scatter(
            grad_gate.astype(jnp.bfloat16), "fsdp", scatter_dimension=0, tiled=True
        ).astype(jnp.float32),
        lax.psum_scatter(
            grad_up.astype(jnp.bfloat16), "fsdp", scatter_dimension=0, tiled=True
        ).astype(jnp.float32),
        lax.psum_scatter(
            grad_down.astype(jnp.bfloat16), "fsdp", scatter_dimension=0, tiled=True
        ).astype(jnp.float32),
    )
    grad_low_one = grad_hidden_one.astype(jnp.bfloat16)
    grad_out_w = jnp.dot(attended_flat.T, grad_low_one, preferred_element_type=jnp.float32)
    attended_gradient = jnp.dot(
        grad_low_one, whole_out.T, preferred_element_type=jnp.float32
    ).astype(jnp.bfloat16)
    attended_gradient = attended_gradient.reshape(
        sequence_count, span_length, QUERY_HEADS * HEAD_DIM
    )
    grad_heads = lax.all_to_all(attended_gradient, "seq", split_axis=2, concat_axis=1, tiled=True)
    full_len = grad_heads.shape[1]
    full_cos, full_sin = rope_tables(jnp.arange(full_len, dtype=jnp.int32), HEAD_DIM)
    back_fn = partial(
        attend_back_item, group_size=group_size, head_size=HEAD_DIM, cosine=full_cos, sine=full_sin
    )
    packed_grads = lax.map(back_fn, (head_inputs, heads_attended, log_totals, grad_heads))
    token_gradients = lax.all_to_all(
        packed_grads, "seq", split_axis=1, concat_axis=2, tiled=True
    ).reshape(row_count, KEY_VALUE_HEADS, group_size + 2, HEAD_DIM)
    grad_queries = token_gradients[:, :, :group_size, :].reshape(row_count, QUERY_HEADS * HEAD_DIM)
    key_gradients = token_gradients[:, :, group_size, :].reshape(
        row_count, KEY_VALUE_HEADS * HEAD_DIM
    )
    value_gradients = token_gradients[:, :, group_size + 1, :].reshape(
        row_count, KEY_VALUE_HEADS * HEAD_DIM
    )
    grad_query = jnp.dot(first_inputs.T, grad_queries, preferred_element_type=jnp.float32)
    grad_key = jnp.dot(first_inputs.T, key_gradients, preferred_element_type=jnp.float32)
    grad_value = jnp.dot(first_inputs.T, value_gradients, preferred_element_type=jnp.float32)
    grad_inputs_one = (
        jnp.dot(grad_queries, whole_query.T, preferred_element_type=jnp.float32)
        + jnp.dot(key_gradients, whole_key.T, preferred_element_type=jnp.float32)
        + jnp.dot(value_gradients, whole_value.T, preferred_element_type=jnp.float32)
    )
    gain_grad_one = jnp.sum(grad_inputs_one * normed_one, axis=0)
    grad_tokens = grad_hidden_one + norm_back(grad_inputs_one, normed_one, inv_one, gain_one)
    attn_shards = (
        lax.psum_scatter(
            gain_grad_one.astype(jnp.bfloat16), "fsdp", scatter_dimension=0, tiled=True
        ).astype(jnp.float32),
        lax.psum_scatter(
            grad_query.astype(jnp.bfloat16), "fsdp", scatter_dimension=0, tiled=True
        ).astype(jnp.float32),
        lax.psum_scatter(
            grad_key.astype(jnp.bfloat16), "fsdp", scatter_dimension=0, tiled=True
        ).astype(jnp.float32),
        lax.psum_scatter(
            grad_value.astype(jnp.bfloat16), "fsdp", scatter_dimension=0, tiled=True
        ).astype(jnp.float32),
        lax.psum_scatter(
            grad_out_w.astype(jnp.bfloat16), "fsdp", scatter_dimension=0, tiled=True
        ).astype(jnp.float32),
    )
    summed = (
        lax.psum(attn_shards[0].astype(jnp.bfloat16), "seq").astype(jnp.float32),
        lax.psum(ffn_shards[0].astype(jnp.bfloat16), "seq").astype(jnp.float32),
        lax.psum(attn_shards[1].astype(jnp.bfloat16), "seq").astype(jnp.float32),
        lax.psum(attn_shards[2].astype(jnp.bfloat16), "seq").astype(jnp.float32),
        lax.psum(attn_shards[3].astype(jnp.bfloat16), "seq").astype(jnp.float32),
        lax.psum(attn_shards[4].astype(jnp.bfloat16), "seq").astype(jnp.float32),
        lax.psum(ffn_shards[1].astype(jnp.bfloat16), "seq").astype(jnp.float32),
        lax.psum(ffn_shards[2].astype(jnp.bfloat16), "seq").astype(jnp.float32),
        lax.psum(ffn_shards[3].astype(jnp.bfloat16), "seq").astype(jnp.float32),
    )
    return (
        block_out.reshape(sequence_count, span_length, width),
        grad_tokens.reshape(sequence_count, span_length, width),
        summed[0],
        summed[1],
        summed[2],
        summed[3],
        summed[4],
        summed[5],
        summed[6],
        summed[7],
        summed[8],
    )


def solution(mesh):
    placed = (
        P("fsdp", "seq", None),
        P("fsdp", "seq", None),
        P("fsdp"),
        P("fsdp"),
        P("fsdp", None),
        P("fsdp", None),
        P("fsdp", None),
        P("fsdp", None),
        P("fsdp", None),
        P("fsdp", None),
        P("fsdp", None),
    )
    return jax.shard_map(
        body,
        mesh=mesh,
        in_specs=placed,
        out_specs=(
            P("fsdp", "seq", None),
            P("fsdp", "seq", None),
            P("fsdp"),
            P("fsdp"),
            P("fsdp", None),
            P("fsdp", None),
            P("fsdp", None),
            P("fsdp", None),
            P("fsdp", None),
            P("fsdp", None),
            P("fsdp", None),
        ),
        check_vma=False,
    )
```

profile of v0, /device:TPU:0, one launch (start us, length us, event | category | flops | bytes accessed | tf_op | source)
XLA Modules:
  0.0 1337.4 jit_solution(4431075528565036426)
XLA Ops:
  13.8 15.5 %all-reduce.5 = (bf16[1536]{0:T(1024)(128)(2,1)S(1)}, bf16[1536]{0:T(1024)(128)(2,1)S(1)}) all-reduce(bf16[1536]{0:T(1024)(128)(2,1)S(1)} %dynamic-update-slice, bf16[1536]{0:T(1024)(128)(2,1)S(1)} %dynamic-update-slice.1), channel_id=1, replica_groups=mesh['seq'=4,'fsdp'=8] {'fsdp'}, use_global_device_ids=true, to_apply=%add | all-reduce | flops 3072 | bytes 12288
  33.0 8.7 all-gather.10.cloned.1.call-done
  48.5 24.0 %all-gather.12.cloned.1.call-done = bf16[1536,768]{1,0:T(8,128)(2,1)} async-done(((bf16[192,768]{1,0:T(8,128)(2,1)}), bf16[1536,768]{1,0:T(8,128)(2,1)}) %all-gather.12.cloned.1.call-update) | async-done | bytes 2359312 | tf_op jit(solution)/shard_map/all_gather | solution.py:147
  78.4 34.8 %all-gather.8.cloned.1.call-done = bf16[1536,1536]{1,0:T(8,128)(2,1)} async-done(((bf16[192,1536]{1,0:T(8,128)(2,1)}), bf16[1536,1536]{1,0:T(8,128)(2,1)}) %all-gather.8.cloned.1.call-update) | async-done | bytes 4718608 | tf_op jit(solution)/shard_map/all_gather | solution.py:145
  113.2 6.8 copy.68
  129.3 4.7 all-to-all-start
  134.1 71.1 %all-to-all-done = bf16[2,256,3072]{1,0,2:T(2,128)(2,1)S(1)} async-done(((bf16[2,256,3072]{1,0,2:T(2,128)(2,1)}), bf16[2,256,3072]{1,0,2:T(2,128)(2,1)S(1)}, u32[]{:S(2)}, u32[]{:S(2)}) %all-to-all-start) | async-done | bytes 3145760 | tf_op jit(solution)/shard_map/all_to_all | solution.py:192
  207.2 4.6 copy.74
  215.1 29.1 %while.25 = (s32[]{:T(128)}, bf16[2,1024,384]{1,2,0:T(8,128)(2,1)}, f32[2,2,2,1024]{3,2,1,0:T(2,128)S(1)}, bf16[2,1024,768]{1,2,0:T(8,128)(2,1)S(1)}, s32[]{:T(128)}) while((s32[]{:T(128)}, bf16[2,1024,384]{1,2,0:T(8,128)(2,1)}, f32[2,2,2,1024]{3,2,1,0:T(2,128)S(1)}, bf16[2,1024,768]{1,2,0:T(8,128)(2,1)S(1)}, s32[]{:T(128)}) %tuple.80), condition=%wide.region_4.5_spmd, body=%wide.region_1.4_spmd.sunk | while | flops 1658187776 | bytes 68026976 | solution.py:77
  222.7 5.9 fusion.110
  237.2 6.0 fusion.110
  244.1 4.9 copy.76
  256.9 33.5 %all-to-all-done.1 = bf16[2,1024,384]{2,0,1:T(2,128)(2,1)} async-done(((bf16[2,1024,384]{2,0,1:T(2,128)(2,1)}), bf16[2,1024,384]{2,0,1:T(2,128)(2,1)}, u32[]{:S(2)}, u32[]{:S(2)}) %all-to-all-start.1) | async-done | bytes 1572896 | tf_op jit(solution)/shard_map/all_to_all | solution.py:194
  294.4 6.5 multiply_reduce_fusion.4
  304.1 12.1 fusion.46
  316.2 12.2 fusion.47
  328.4 46.9 %all-gather.20.cloned.1.call-done = bf16[4096,1536]{1,0:T(8,128)(2,1)} async-done(((bf16[512,1536]{1,0:T(8,128)(2,1)}), bf16[4096,1536]{1,0:T(8,128)(2,1)}) %all-gather.20.cloned.1.call-update) | async-done | bytes 12582928 | tf_op jit(solution)/shard_map/all_gather | solution.py:213
  375.2 19.2 %multiply_convert_fusion = (bf16[512,4096]{1,0:T(8,128)(2,1)}, bf16[512,4096]{1,0:T(8,128)(2,1)}, bf16[512,4096]{1,0:T(8,128)(2,1)}) fusion(f32[512,4096]{1,0:T(8,128)} %fusion.46, f32[512,4096]{1,0:T(8,128)} %fusion.47, bf16[512,1536]{1,0:T(8,128)(2,1)} %bitcast_convert_fusion, bf16[4096,1536]{1,0:T(8,128)(2,1)} %all-gather.20.cloned.1.call-done), kind=kOutput, calls=%fused_computation.61 | convolution fusion | flops 6476005376 | bytes 43515904 | tf_op jit(solution)/shard_map/dot_general | solution.py:220
  394.4 11.2 fusion.48
  405.7 12.0 multiply_reduce_fusion
  418.4 7.3 convolution_convert_fusion.7
  425.7 4.9 copy.78
  435.2 7.1 convolution_convert_fusion.3
  442.4 30.3 %all-to-all-done.2 = bf16[2,256,1536]{1,0,2:T(2,128)(2,1)} async-done(((bf16[2,256,1536]{1,0,2:T(2,128)(2,1)}), bf16[2,256,1536]{1,0,2:T(2,128)(2,1)}, u32[]{:S(2)}, u32[]{:S(2)}) %all-to-all-start.2) | async-done | bytes 1572896 | tf_op jit(solution)/shard_map/all_to_all | solution.py:262
  480.3 73.4 %while.26 = (s32[]{:T(128)}, bf16[2,1024,768]{1,2,0:T(8,128)(2,1)}, bf16[2,1024,768]{1,2,0:T(8,128)(2,1)S(1)}, f32[2,2,2,1024]{3,2,1,0:T(2,128)S(1)}, bf16[2,102...) while((s32[]{:T(128)}, bf16[2,1024,768]{1,2,0:T(8,128)(2,1)}, ...), condition=%wide.region_8.9_spmd.clone.clone.clone, body=%wide.region_7.8_spmd.clone.clone.clone.sunk | while | flops 4085755904 | bytes 115446648 | solution.py:268
  482.4 8.3 fusion.118
  491.0 10.1 fusion.121
  507.3 8.3 fusion.119
  518.9 8.1 fusion.118
  527.4 10.0 fusion.121
  543.6 8.3 fusion.119
  553.6 7.6 copy.81
  561.3 73.6 %all_to_all.66 = bf16[2,1024,768]{2,0,1:T(2,128)(2,1)} all-to-all(bf16[2,1024,768]{2,0,1:T(2,128)(2,1)S(1)} %copy.81), channel_id=1, replica_groups=mesh['seq'=4,'fsdp'=8] {'seq'}, dimensions={1} | all-to-all | bytes 6291456 | tf_op jit(solution)/shard_map/all_to_all | solution.py:269
  634.9 11.2 copy.82
  667.9 11.8 convolution_convert_fusion.2
  679.8 11.9 convolution_convert_fusion.1
  693.1 11.9 convolution_convert_fusion
  705.1 37.1 %reduce-scatter.12.cloned.1.call-done = bf16[192,768]{1,0:T(8,128)(2,1)} async-done(((bf16[1536,768]{1,0:T(8,128)(2,1)}), bf16[192,768]{1,0:T(8,128)(2,1)}) %reduce-scatter.12.cloned.1.call-update) | async-done | bytes 294928 | tf_op jit(solution)/shard_map/reduce_scatter | solution.py:299
  742.2 57.3 %reduce-scatter.8.cloned.1.call-done = bf16[192,1536]{1,0:T(8,128)(2,1)} async-done(((bf16[1536,1536]{1,0:T(8,128)(2,1)}), bf16[192,1536]{1,0:T(8,128)(2,1)}) %reduce-scatter.8.cloned.1.call-update) | async-done | bytes 589840 | tf_op jit(solution)/shard_map/reduce_scatter | solution.py:293
  799.5 95.7 %reduce-scatter.16.cloned.1.call-done = bf16[192,4096]{1,0:T(8,128)(2,1)} async-done(((bf16[1536,4096]{1,0:T(8,128)(2,1)}), bf16[192,4096]{1,0:T(8,128)(2,1)}) %reduce-scatter.16.cloned.1.call-update) | async-done | bytes 1572880 | tf_op jit(solution)/shard_map/reduce_scatter | solution.py:244
  895.2 95.8 %reduce-scatter.18.cloned.1.call-done = bf16[192,4096]{1,0:T(8,128)(2,1)} async-done(((bf16[1536,4096]{1,0:T(8,128)(2,1)}), bf16[192,4096]{1,0:T(8,128)(2,1)}) %reduce-scatter.18.cloned.1.call-update) | async-done | bytes 1572880 | tf_op jit(solution)/shard_map/reduce_scatter | solution.py:247
  991.0 95.7 %reduce-scatter.20.cloned.1.call-done = bf16[512,1536]{1,0:T(8,128)(2,1)} async-done(((bf16[4096,1536]{1,0:T(8,128)(2,1)}), bf16[512,1536]{1,0:T(8,128)(2,1)}) %reduce-scatter.20.cloned.1.call-update) | async-done | bytes 1572880 | tf_op jit(solution)/shard_map/reduce_scatter | solution.py:250
  1088.5 12.2 convolution_add_fusion.3
  1100.8 4.7 fusion.49
  1112.1 13.6 %all-reduce.4 = (bf16[1536]{0:T(1024)(128)(2,1)S(1)}, bf16[1536]{0:T(1024)(128)(2,1)S(1)}) all-reduce(bf16[1536]{0:T(1024)(128)(2,1)S(1)} %get-tuple-element.208, bf16[1536]{0:T(1024)(128)(2,1)S(1)} %copy-done.38), channel_id=2, replica_groups=mesh['seq'=4,'fsdp'=8] {'fsdp'}, use_global_device_ids=true, to_apply=%region_11.12.clone | all-reduce | flops 3072 | bytes 12288
  1125.8 12.3 all-reduce.6
  1139.2 5.3 multiply_add_fusion
  1144.5 174.5 %all-reduce.10.cloned.1.call-done = (bf16[192,1536]{1,0:T(8,128)(2,1)}, bf16[192,768]{1,0:T(8,128)(2,1)}, bf16[192,768]{1,0:T(8,128)(2,1)}, bf16[192,1536]{1,0:T...) async-done(((bf16[192,1536]{1,0:T(8,128)(2,1)}, bf16[192,768]{1,0:T(8,128)(2,1)}, bf16[192,768]{1,0:T(8,128)(2,1)}, ...) | async-done | bytes 6488080 | tf_op jit(solution)/shard_map/psum | solution.py:309
  (229 shorter events, 145.0 us)
Async XLA Ops:
  7.2 34.6 %all-gather.10.cloned.1.call-start = ((), (), s32[]{:S(2)}) async-start(), calls=%async_computation.12 | async-start | bytes 2654208 | tf_op jit(solution)/shard_map/all_gather | solution.py:146
  7.9 4.1 copy-start.39
  7.9 5.4 copy-start.40
  7.9 5.6 copy-start.41
  7.9 21.4 %copy-start = (f32[2,256,1536]{2,1,0:T(8,128)S(1)}, f32[2,256,1536]{2,1,0:T(8,128)}, u32[]{:S(2)}) copy-start(f32[2,256,1536]{2,1,0:T(8,128)} %param.15) | copy-start | bytes 9437188
  8.0 64.6 %all-gather.12.cloned.1.call-start = ((), (), s32[]{:S(2)}) async-start(), calls=%async_computation.13 | async-start | bytes 2654208 | tf_op jit(solution)/shard_map/all_gather | solution.py:147
  8.7 104.5 %all-gather.8.cloned.1.call-start = ((), (), s32[]{:S(2)}) async-start(), calls=%async_computation.11 | async-start | bytes 5308416 | tf_op jit(solution)/shard_map/all_gather | solution.py:145
  9.4 285.0 %all-gather.14.cloned.1.call-start = ((), (), s32[]{:S(2)}) async-start(), calls=%async_computation.14 | async-start | bytes 5308416 | tf_op jit(solution)/shard_map/all_gather | solution.py:148
  10.0 294.1 %all-gather.16.cloned.1.call-start = ((), (), s32[]{:S(2)}) async-start(), calls=%async_computation.15 | async-start | bytes 14155776 | tf_op jit(solution)/shard_map/all_gather | solution.py:202
  10.6 305.6 %all-gather.18.cloned.1.call-start = ((), (), s32[]{:S(2)}) async-start(), calls=%async_computation.16 | async-start | bytes 14155776 | tf_op jit(solution)/shard_map/all_gather | solution.py:203
  11.2 364.1 %all-gather.20.cloned.1.call-start = ((), (), s32[]{:S(2)}) async-start(), calls=%async_computation.17 | async-start | bytes 14155776 | tf_op jit(solution)/shard_map/all_gather | solution.py:213
  12.0 18.0 %copy-start.36 = (f32[48]{0:T(128)}, f32[48]{0:T(128)S(1)}, u32[]{:S(2)}) copy-start(f32[48]{0:T(128)S(1)} %multiply_power_fusion) | copy-start | bytes 580
  48.5 28.7 %copy-start.20 = (f32[512,8,96]{0,2,1:T(8,128)S(1)}, f32[512,8,96]{0,2,1:T(8,128)}, u32[]{:S(2)}) copy-start(f32[512,8,96]{0,2,1:T(8,128)} %fusion.45) | copy-start | bytes 4718596
  113.2 6.8 copy-start.21
  129.3 75.8 %all-to-all-start = ((bf16[2,256,3072]{1,0,2:T(2,128)(2,1)}), bf16[2,256,3072]{1,0,2:T(2,128)(2,1)S(1)}, u32[]{:S(2)}, u32[]{:S(2)}) async-start(bf16[2,256,3072]{1,0,2:T(2,128)(2,1)} %reshape.346), calls=%async_computation | async-start | bytes 6291456 | tf_op jit(solution)/shard_map/all_to_all | solution.py:192
  215.2 3.8 copy-start.2
  229.7 3.8 copy-start.2
  249.1 41.3 %all-to-all-start.1 = ((bf16[2,1024,384]{2,0,1:T(2,128)(2,1)}), bf16[2,1024,384]{2,0,1:T(2,128)(2,1)}, u32[]{:S(2)}, u32[]{:S(2)}) async-start(bf16[2,1024,384]{2,0,1:T(2,128)(2,1)} %copy.76), calls=%async_computation.1 | async-start | bytes 3145728 | tf_op jit(solution)/shard_map/all_to_all | solution.py:194
  394.4 11.2 copy-start.9
  405.6 12.0 copy-start.6
  418.4 7.3 copy-start.7
  430.6 42.1 %all-to-all-start.2 = ((bf16[2,256,1536]{1,0,2:T(2,128)(2,1)}), bf16[2,256,1536]{1,0,2:T(2,128)(2,1)}, u32[]{:S(2)}, u32[]{:S(2)}) async-start(bf16[2,256,1536]{1,0,2:T(2,128)(2,1)} %copy.78), calls=%async_computation.2 | async-start | bytes 3145728 | tf_op jit(solution)/shard_map/all_to_all | solution.py:262
  435.2 270.0 %reduce-scatter.14.cloned.1.call-start = ((), (), s32[]{:S(2)}) async-start(), calls=%async_computation.21 | async-start | bytes 5308416 | tf_op jit(solution)/shard_map/reduce_scatter | solution.py:302
  442.3 262.8 %reduce-scatter.10.cloned.1.call-start = ((), (), s32[]{:S(2)}) async-start(), calls=%async_computation.19 | async-start | bytes 2654208 | tf_op jit(solution)/shard_map/reduce_scatter | solution.py:296
  472.6 7.6 copy-start.37
  491.0 10.2 copy-start.4
  504.4 2.9 copy-start.5
  507.3 8.3 copy-start.3
  527.4 10.0 copy-start.4
  540.7 2.9 copy-start.5
  543.6 8.3 copy-start.3
  655.4 86.8 %reduce-scatter.12.cloned.1.call-start = ((), (), s32[]{:S(2)}) async-start(), calls=%async_computation.20 | async-start | bytes 2654208 | tf_op jit(solution)/shard_map/reduce_scatter | solution.py:299
  659.9 139.6 %reduce-scatter.8.cloned.1.call-start = ((), (), s32[]{:S(2)}) async-start(), calls=%async_computation.18 | async-start | bytes 5308416 | tf_op jit(solution)/shard_map/reduce_scatter | solution.py:293
  666.5 228.7 %reduce-scatter.16.cloned.1.call-start = ((), (), s32[]{:S(2)}) async-start(), calls=%async_computation.22 | async-start | bytes 14155776 | tf_op jit(solution)/shard_map/reduce_scatter | solution.py:244
  679.8 311.2 %reduce-scatter.18.cloned.1.call-start = ((), (), s32[]{:S(2)}) async-start(), calls=%async_computation.23 | async-start | bytes 14155776 | tf_op jit(solution)/shard_map/reduce_scatter | solution.py:247
  691.7 394.9 %reduce-scatter.20.cloned.1.call-start = ((), (), s32[]{:S(2)}) async-start(), calls=%async_computation.24 | async-start | bytes 14155776 | tf_op jit(solution)/shard_map/reduce_scatter | solution.py:250
  705.0 614.0 %all-reduce.10.cloned.1.call-start = ((), (), s32[]{:S(2)}) async-start(), calls=%async_computation.25 | async-start | bytes 12976128 | tf_op jit(solution)/shard_map/psum | solution.py:309
  1088.5 12.2 copy-start.19
  1100.8 4.7 copy-start.11
  1100.8 4.7 copy-start.16
  1105.6 2.8 copy-start.17
  1105.6 2.8 copy-start.33
  1105.6 2.8 copy-start.35
  1108.4 3.7 copy-start.38
  1319.1 3.6 copy-start.27
  1324.6 3.2 copy-start.28
  1324.6 4.4 copy-start.31
  1326.7 3.2 copy-start.30
  (16 other events, 26.7 us)
Sparse Core Ops, SparseCore 0:
  9.9 31.8 all-gather.9
  43.6 28.8 all-gather.11
  74.4 38.7 all-gather.7
  115.0 38.7 all-gather.13
  155.5 71.9 all-gather.15
  229.3 71.9 all-gather.17
  303.2 71.9 all-gather.19
  442.5 54.2 reduce-scatter.13
  655.5 40.4 reduce-scatter.9
  699.8 42.3 reduce-scatter.11
  745.7 53.7 reduce-scatter.7
  802.8 92.2 reduce-scatter.15
  898.7 92.2 reduce-scatter.17
  994.3 92.2 reduce-scatter.19
  1089.4 229.5 all-reduce.9
where the time goes:
time: 1340 us
  waiting for transfers between devices  810 us (60%)
  matrix products  249 us (19%)
  blocking collectives  115 us (9%)
  local copies, waits for them, and re-layouts  89.6 us (7%)
  other arithmetic  42.4 us (3%)
  between operations  16.2 us (1%)
  starting transfers between devices  14.4 us (1%)
    psum x1, waiting for transfers between devices, body(): lax.psum(attn_shards[1].astype(jnp.bfloat16), 'seq').astype(jnp.float32)  175 us
    reduce_scatter x1, waiting for transfers between devices, body(): lax.psum_scatter(grad_up.astype(jnp.bfloat16), 'fsdp', scatter_dimension=...  95.8 us
    reduce_scatter x1, waiting for transfers between devices, body(): lax.psum_scatter(grad_gate.astype(jnp.bfloat16), 'fsdp', scatter_dimensio...  95.7 us
    reduce_scatter x1, waiting for transfers between devices, body(): lax.psum_scatter(grad_down.astype(jnp.bfloat16), 'fsdp', scatter_dimensio...  95.7 us
    all_to_all x1, blocking collectives, body(): lax.all_to_all(packed_grads, 'seq', split_axis=1, concat_axis=2, tiled=True)  73.6 us
    all_to_all x1, waiting for transfers between devices, body(): lax.all_to_all(packed_arrays, 'seq', split_axis=2, concat_axis=1, tiled=T...  71.1 us
    reduce_scatter x1, waiting for transfers between devices, body(): lax.psum_scatter(grad_query.astype(jnp.bfloat16), 'fsdp', scatter_dimensi...  57.3 us
    all_gather x1, waiting for transfers between devices, body(): lax.all_gather(down_weight, 'fsdp', axis=0, tiled=True)  46.9 us
  transfers between devices with their start and end apart: 18, of which 13 were waited for; matrix products, arithmetic and copies ran while one was open for 22% of the time, Pallas kernels for 0%

commit v1 on v0

--- a/solution.py
+++ b/solution.py
@@ -306,7 +306,9 @@
     summed = (
         lax.psum(attn_shards[0].astype(jnp.bfloat16), "seq").astype(jnp.float32),
         lax.psum(ffn_shards[0].astype(jnp.bfloat16), "seq").astype(jnp.float32),
-        lax.psum(attn_shards[1].astype(jnp.bfloat16), "seq").astype(jnp.float32),
+        jnp.sum(jax.lax.all_gather(attn_shards[1].astype(jnp.bfloat16), axis_name="seq"), 0).astype(
+            jnp.float32
+        ),
         lax.psum(attn_shards[2].astype(jnp.bfloat16), "seq").astype(jnp.float32),
         lax.psum(attn_shards[3].astype(jnp.bfloat16), "seq").astype(jnp.float32),
         lax.psum(attn_shards[4].astype(jnp.bfloat16), "seq").astype(jnp.float32),

time: 1340 us -> 1430 us (1.067)
  waiting for transfers between devices: 810 us -> 899 us
    reduce_scatter x1, waiting for transfers between devices: 57.3 us -> 0.02 us  [body(): lax.psum_scatter(grad_query.astype(jnp.bfloat16), 'fsdp', scatter_dimensi...]
    reduce_scatter x1, waiting for transfers between devices: 0.02 us -> 54.6 us  [body(): lax.psum_scatter(grad_out_w.astype(jnp.bfloat16), 'fsdp', scatter_dimensi...]
    reduce_scatter x1, waiting for transfers between devices: 0.02 us -> 46.1 us  [body(): lax.psum_scatter(grad_key.astype(jnp.bfloat16), 'fsdp', scatter_dimension...]
    psum x1, waiting for transfers between devices: 175 us -> 203 us  [body(): lax.psum(attn_shards[2].astype(jnp.bfloat16), 'seq').astype(jnp.float32)]
  transfers between devices with their start and end apart: 18 -> 19, of which waited for: 13 -> 14; matrix products, arithmetic and copies ran while one was open for 22% -> 14% of each run, Pallas kernels for 0% -> 0%
where the time goes in v1:
time: 1430 us
  waiting for transfers between devices  899 us (63%)
  matrix products  248 us (17%)
  blocking collectives  115 us (8%)
  local copies, waits for them, and re-layouts  88.4 us (6%)
  other arithmetic  44.6 us (3%)
  between operations  16.2 us (1%)
  starting transfers between devices  14.7 us (1%)
    psum x1, waiting for transfers between devices, body(): lax.psum(attn_shards[2].astype(jnp.bfloat16), 'seq').astype(jnp.float32)  203 us
    reduce_scatter x1, waiting for transfers between devices, body(): lax.psum_scatter(grad_up.astype(jnp.bfloat16), 'fsdp', scatter_dimension=...  95.8 us
    reduce_scatter x1, waiting for transfers between devices, body(): lax.psum_scatter(grad_gate.astype(jnp.bfloat16), 'fsdp', scatter_dimensio...  95.7 us
    reduce_scatter x1, waiting for transfers between devices, body(): lax.psum_scatter(grad_down.astype(jnp.bfloat16), 'fsdp', scatter_dimensio...  95.7 us
    all_to_all x1, blocking collectives, body(): lax.all_to_all(packed_grads, 'seq', split_axis=1, concat_axis=2, tiled=True)  73.6 us
    all_to_all x1, waiting for transfers between devices, body(): lax.all_to_all(packed_arrays, 'seq', split_axis=2, concat_axis=1, tiled=T...  71.1 us
    reduce_scatter x1, waiting for transfers between devices, body(): lax.psum_scatter(grad_out_w.astype(jnp.bfloat16), 'fsdp', scatter_dimensi...  54.6 us
    all_gather x1, waiting for transfers between devices, body(): lax.all_gather(down_weight, 'fsdp', axis=0, tiled=True)  46.8 us
  transfers between devices with their start and end apart: 19, of which 14 were waited for; matrix products, arithmetic and copies ran while one was open for 14% of the time, Pallas kernels for 0%

profile of v1, /device:TPU:0, one launch (start us, length us, event | category | flops | bytes accessed | tf_op | source)
XLA Modules:
  0.0 1426.6 jit_solution(10523342368372629418)
XLA Ops:
  13.8 15.5 %all-reduce.5 = (bf16[1536]{0:T(1024)(128)(2,1)S(1)}, bf16[1536]{0:T(1024)(128)(2,1)S(1)}) all-reduce(bf16[1536]{0:T(1024)(128)(2,1)S(1)} %dynamic-update-slice, bf16[1536]{0:T(1024)(128)(2,1)S(1)} %dynamic-update-slice.1), channel_id=1, replica_groups=mesh['seq'=4,'fsdp'=8] {'fsdp'}, use_global_device_ids=true, to_apply=%add | all-reduce | flops 3072 | bytes 12288
  33.0 8.7 all-gather.12.cloned.1.call-done
  48.5 24.0 %all-gather.14.cloned.1.call-done = bf16[1536,768]{1,0:T(8,128)(2,1)} async-done(((bf16[192,768]{1,0:T(8,128)(2,1)}), bf16[1536,768]{1,0:T(8,128)(2,1)}) %all-gather.14.cloned.1.call-update) | async-done | bytes 2359312 | tf_op jit(solution)/shard_map/all_gather | solution.py:147
  78.4 34.8 %all-gather.10.cloned.1.call-done = bf16[1536,1536]{1,0:T(8,128)(2,1)} async-done(((bf16[192,1536]{1,0:T(8,128)(2,1)}), bf16[1536,1536]{1,0:T(8,128)(2,1)}) %all-gather.10.cloned.1.call-update) | async-done | bytes 4718608 | tf_op jit(solution)/shard_map/all_gather | solution.py:145
  113.2 6.8 copy.68
  129.3 5.0 all-to-all-start
  134.3 71.1 %all-to-all-done = bf16[2,256,3072]{1,0,2:T(2,128)(2,1)S(1)} async-done(((bf16[2,256,3072]{1,0,2:T(2,128)(2,1)}), bf16[2,256,3072]{1,0,2:T(2,128)(2,1)S(1)}, u32[]{:S(2)}, u32[]{:S(2)}) %all-to-all-start) | async-done | bytes 3145760 | tf_op jit(solution)/shard_map/all_to_all | solution.py:192
  215.3 29.1 %while.25 = (s32[]{:T(128)}, bf16[2,1024,384]{1,2,0:T(8,128)(2,1)}, f32[2,2,2,1024]{3,2,1,0:T(2,128)S(1)}, bf16[2,1024,768]{1,2,0:T(8,128)(2,1)S(1)}, s32[]{:T(128)}) while((s32[]{:T(128)}, bf16[2,1024,384]{1,2,0:T(8,128)(2,1)}, f32[2,2,2,1024]{3,2,1,0:T(2,128)S(1)}, bf16[2,1024,768]{1,2,0:T(8,128)(2,1)S(1)}, s32[]{:T(128)}) %tuple.80), condition=%wide.region_4.5_spmd, body=%wide.region_1.4_spmd.sunk | while | flops 1658187776 | bytes 68026976 | solution.py:77
  222.9 5.9 fusion.110
  237.4 6.0 fusion.110
  244.4 4.9 copy.76
  257.1 33.4 %all-to-all-done.1 = bf16[2,1024,384]{2,0,1:T(2,128)(2,1)} async-done(((bf16[2,1024,384]{2,0,1:T(2,128)(2,1)}), bf16[2,1024,384]{2,0,1:T(2,128)(2,1)}, u32[]{:S(2)}, u32[]{:S(2)}) %all-to-all-start.1) | async-done | bytes 1572896 | tf_op jit(solution)/shard_map/all_to_all | solution.py:194
  294.5 6.5 multiply_reduce_fusion.4
  304.2 12.2 fusion.46
  316.4 12.1 fusion.47
  328.5 46.8 %all-gather.22.cloned.1.call-done = bf16[4096,1536]{1,0:T(8,128)(2,1)} async-done(((bf16[512,1536]{1,0:T(8,128)(2,1)}), bf16[4096,1536]{1,0:T(8,128)(2,1)}) %all-gather.22.cloned.1.call-update) | async-done | bytes 12582928 | tf_op jit(solution)/shard_map/all_gather | solution.py:213
  375.3 19.2 %multiply_convert_fusion = (bf16[512,4096]{1,0:T(8,128)(2,1)}, bf16[512,4096]{1,0:T(8,128)(2,1)}, bf16[512,4096]{1,0:T(8,128)(2,1)}) fusion(f32[512,4096]{1,0:T(8,128)} %fusion.46, f32[512,4096]{1,0:T(8,128)} %fusion.47, bf16[512,1536]{1,0:T(8,128)(2,1)} %bitcast_convert_fusion, bf16[4096,1536]{1,0:T(8,128)(2,1)} %all-gather.22.cloned.1.call-done), kind=kOutput, calls=%fused_computation.61 | convolution fusion | flops 6476005376 | bytes 43515904 | tf_op jit(solution)/shard_map/dot_general | solution.py:220
  394.5 10.9 fusion.48
  405.5 12.0 multiply_reduce_fusion
  418.2 7.3 convolution_convert_fusion.7
  425.5 4.9 copy.78
  435.0 37.5 %all-to-all-done.2 = bf16[2,256,1536]{1,0,2:T(2,128)(2,1)} async-done(((bf16[2,256,1536]{1,0,2:T(2,128)(2,1)}), bf16[2,256,1536]{1,0,2:T(2,128)(2,1)}, u32[]{:S(2)}, u32[]{:S(2)}) %all-to-all-start.2) | async-done | bytes 1572896 | tf_op jit(solution)/shard_map/all_to_all | solution.py:262
  480.1 73.1 %while.26 = (s32[]{:T(128)}, bf16[2,1024,768]{1,2,0:T(8,128)(2,1)}, bf16[2,1024,768]{1,2,0:T(8,128)(2,1)S(1)}, f32[2,2,2,1024]{3,2,1,0:T(2,128)S(1)}, bf16[2,102...) while((s32[]{:T(128)}, bf16[2,1024,768]{1,2,0:T(8,128)(2,1)}, ...), condition=%wide.region_8.9_spmd.clone.clone.clone, body=%wide.region_7.8_spmd.clone.clone.clone.sunk | while | flops 4085755904 | bytes 115446648 | solution.py:268
  482.5 8.2 fusion.118
  491.0 10.0 fusion.121
  507.2 8.3 fusion.119
  518.8 8.2 fusion.118
  527.2 10.0 fusion.121
  543.5 8.3 fusion.119
  553.3 7.6 copy.81
  560.9 73.6 %all_to_all.66 = bf16[2,1024,768]{2,0,1:T(2,128)(2,1)} all-to-all(bf16[2,1024,768]{2,0,1:T(2,128)(2,1)S(1)} %copy.81), channel_id=1, replica_groups=mesh['seq'=4,'fsdp'=8] {'seq'}, dimensions={1} | all-to-all | bytes 6291456 | tf_op jit(solution)/shard_map/all_to_all | solution.py:269
  634.5 11.2 copy.82
  656.8 7.3 convolution_convert_fusion.3
  671.9 11.7 convolution_convert_fusion.2
  685.1 12.0 convolution_convert_fusion.1
  698.5 12.3 convolution_convert_fusion
  711.5 54.6 %reduce-scatter.14.cloned.1.call-done = bf16[192,1536]{1,0:T(8,128)(2,1)} async-done(((bf16[1536,1536]{1,0:T(8,128)(2,1)}), bf16[192,1536]{1,0:T(8,128)(2,1)}) %reduce-scatter.14.cloned.1.call-update) | async-done | bytes 589840 | tf_op jit(solution)/shard_map/reduce_scatter | solution.py:302
  766.1 46.1 %reduce-scatter.10.cloned.1.call-done = bf16[192,768]{1,0:T(8,128)(2,1)} async-done(((bf16[1536,768]{1,0:T(8,128)(2,1)}), bf16[192,768]{1,0:T(8,128)(2,1)}) %reduce-scatter.10.cloned.1.call-update) | async-done | bytes 294928 | tf_op jit(solution)/shard_map/reduce_scatter | solution.py:296
  812.2 46.3 %reduce-scatter.12.cloned.1.call-done = bf16[192,768]{1,0:T(8,128)(2,1)} async-done(((bf16[1536,768]{1,0:T(8,128)(2,1)}), bf16[192,768]{1,0:T(8,128)(2,1)}) %reduce-scatter.12.cloned.1.call-update) | async-done | bytes 294928 | tf_op jit(solution)/shard_map/reduce_scatter | solution.py:299
  858.5 95.7 %reduce-scatter.16.cloned.1.call-done = bf16[192,4096]{1,0:T(8,128)(2,1)} async-done(((bf16[1536,4096]{1,0:T(8,128)(2,1)}), bf16[192,4096]{1,0:T(8,128)(2,1)}) %reduce-scatter.16.cloned.1.call-update) | async-done | bytes 1572880 | tf_op jit(solution)/shard_map/reduce_scatter | solution.py:244
  954.2 95.8 %reduce-scatter.18.cloned.1.call-done = bf16[192,4096]{1,0:T(8,128)(2,1)} async-done(((bf16[1536,4096]{1,0:T(8,128)(2,1)}), bf16[192,4096]{1,0:T(8,128)(2,1)}) %reduce-scatter.18.cloned.1.call-update) | async-done | bytes 1572880 | tf_op jit(solution)/shard_map/reduce_scatter | solution.py:247
  1050.0 95.7 %reduce-scatter.20.cloned.1.call-done = bf16[512,1536]{1,0:T(8,128)(2,1)} async-done(((bf16[4096,1536]{1,0:T(8,128)(2,1)}), bf16[512,1536]{1,0:T(8,128)(2,1)}) %reduce-scatter.20.cloned.1.call-update) | async-done | bytes 1572880 | tf_op jit(solution)/shard_map/reduce_scatter | solution.py:250
  1146.3 12.4 convolution_add_fusion.3
  1158.7 4.7 fusion.49
  1170.0 13.6 all-reduce.4
  1183.8 12.2 all-reduce.6
  1197.1 5.2 multiply_add_fusion
  1205.7 203.4 %all-reduce.10.cloned.1.call-done = (bf16[192,768]{1,0:T(8,128)(2,1)}, bf16[192,768]{1,0:T(8,128)(2,1)}, bf16[192,1536]{1,0:T(8,128)(2,1)}, bf16[192,4096]{1,0:T...) async-done(((bf16[192,768]{1,0:T(8,128)(2,1)}, bf16[192,768]{1,0:T(8,128)(2,1)}, bf16[192,1536]{1,0:T(8,128)(2,1)}, bf16[192,4096]{1,0:T(8,128)(2,1)}, ...) | async-done | bytes 5898256 | tf_op jit(solution)/shard_map/psum | solution.py:312
  (235 shorter events, 149.7 us)
Async XLA Ops:
  7.2 34.6 %all-gather.12.cloned.1.call-start = ((), (), s32[]{:S(2)}) async-start(), calls=%async_computation.12 | async-start | bytes 2654208 | tf_op jit(solution)/shard_map/all_gather | solution.py:146
  7.9 4.1 copy-start.40
  7.9 5.3 copy-start.41
  7.9 5.6 copy-start.42
  7.9 21.4 %copy-start = (f32[2,256,1536]{2,1,0:T(8,128)S(1)}, f32[2,256,1536]{2,1,0:T(8,128)}, u32[]{:S(2)}) copy-start(f32[2,256,1536]{2,1,0:T(8,128)} %param.15) | copy-start | bytes 9437188
  8.0 64.6 %all-gather.14.cloned.1.call-start = ((), (), s32[]{:S(2)}) async-start(), calls=%async_computation.13 | async-start | bytes 2654208 | tf_op jit(solution)/shard_map/all_gather | solution.py:147
  8.7 104.5 %all-gather.10.cloned.1.call-start = ((), (), s32[]{:S(2)}) async-start(), calls=%async_computation.11 | async-start | bytes 5308416 | tf_op jit(solution)/shard_map/all_gather | solution.py:145
  9.4 285.1 %all-gather.16.cloned.1.call-start = ((), (), s32[]{:S(2)}) async-start(), calls=%async_computation.14 | async-start | bytes 5308416 | tf_op jit(solution)/shard_map/all_gather | solution.py:148
  10.0 294.2 %all-gather.18.cloned.1.call-start = ((), (), s32[]{:S(2)}) async-start(), calls=%async_computation.15 | async-start | bytes 14155776 | tf_op jit(solution)/shard_map/all_gather | solution.py:202
  10.6 305.8 %all-gather.20.cloned.1.call-start = ((), (), s32[]{:S(2)}) async-start(), calls=%async_computation.16 | async-start | bytes 14155776 | tf_op jit(solution)/shard_map/all_gather | solution.py:203
  11.2 364.1 %all-gather.22.cloned.1.call-start = ((), (), s32[]{:S(2)}) async-start(), calls=%async_computation.17 | async-start | bytes 14155776 | tf_op jit(solution)/shard_map/all_gather | solution.py:213
  12.0 18.0 %copy-start.37 = (f32[48]{0:T(128)}, f32[48]{0:T(128)S(1)}, u32[]{:S(2)}) copy-start(f32[48]{0:T(128)S(1)} %multiply_power_fusion) | copy-start | bytes 580
  48.5 28.7 %copy-start.21 = (f32[512,8,96]{0,2,1:T(8,128)S(1)}, f32[512,8,96]{0,2,1:T(8,128)}, u32[]{:S(2)}) copy-start(f32[512,8,96]{0,2,1:T(8,128)} %fusion.45) | copy-start | bytes 4718596
  113.2 6.8 copy-start.22
  129.3 76.1 %all-to-all-start = ((bf16[2,256,3072]{1,0,2:T(2,128)(2,1)}), bf16[2,256,3072]{1,0,2:T(2,128)(2,1)S(1)}, u32[]{:S(2)}, u32[]{:S(2)}) async-start(bf16[2,256,3072]{1,0,2:T(2,128)(2,1)} %reshape.346), calls=%async_computation | async-start | bytes 6291456 | tf_op jit(solution)/shard_map/all_to_all | solution.py:192
  215.4 3.8 copy-start.2
  230.0 3.8 copy-start.2
  249.3 41.2 %all-to-all-start.1 = ((bf16[2,1024,384]{2,0,1:T(2,128)(2,1)}), bf16[2,1024,384]{2,0,1:T(2,128)(2,1)}, u32[]{:S(2)}, u32[]{:S(2)}) async-start(bf16[2,1024,384]{2,0,1:T(2,128)(2,1)} %copy.76), calls=%async_computation.1 | async-start | bytes 3145728 | tf_op jit(solution)/shard_map/all_to_all | solution.py:194
  394.5 11.0 copy-start.9
  405.4 12.0 copy-start.6
  418.2 7.3 copy-start.7
  430.4 42.1 %all-to-all-start.2 = ((bf16[2,256,1536]{1,0,2:T(2,128)(2,1)}), bf16[2,256,1536]{1,0,2:T(2,128)(2,1)}, u32[]{:S(2)}, u32[]{:S(2)}) async-start(bf16[2,256,1536]{1,0,2:T(2,128)(2,1)} %copy.78), calls=%async_computation.2 | async-start | bytes 3145728 | tf_op jit(solution)/shard_map/all_to_all | solution.py:262
  435.0 275.9 %reduce-scatter.8.cloned.1.call-start = ((), (), s32[]{:S(2)}) async-start(), calls=%async_computation.18 | async-start | bytes 5308416 | tf_op jit(solution)/shard_map/reduce_scatter | solution.py:293
  472.5 7.7 copy-start.38
  490.9 10.0 copy-start.4
  504.2 2.9 copy-start.5
  507.2 8.3 copy-start.3
  527.2 10.0 copy-start.4
  540.5 2.9 copy-start.5
  543.4 8.3 copy-start.3
  656.7 109.3 %reduce-scatter.14.cloned.1.call-start = ((), (), s32[]{:S(2)}) async-start(), calls=%async_computation.21 | async-start | bytes 5308416 | tf_op jit(solution)/shard_map/reduce_scatter | solution.py:302
  664.1 148.2 %reduce-scatter.10.cloned.1.call-start = ((), (), s32[]{:S(2)}) async-start(), calls=%async_computation.19 | async-start | bytes 2654208 | tf_op jit(solution)/shard_map/reduce_scatter | solution.py:296
  666.0 2.9 copy-start.14
  666.0 2.9 copy-start.25
  668.9 189.6 %reduce-scatter.12.cloned.1.call-start = ((), (), s32[]{:S(2)}) async-start(), calls=%async_computation.20 | async-start | bytes 2654208 | tf_op jit(solution)/shard_map/reduce_scatter | solution.py:299
  671.8 282.4 %reduce-scatter.16.cloned.1.call-start = ((), (), s32[]{:S(2)}) async-start(), calls=%async_computation.22 | async-start | bytes 14155776 | tf_op jit(solution)/shard_map/reduce_scatter | solution.py:244
  683.7 366.4 %reduce-scatter.18.cloned.1.call-start = ((), (), s32[]{:S(2)}) async-start(), calls=%async_computation.23 | async-start | bytes 14155776 | tf_op jit(solution)/shard_map/reduce_scatter | solution.py:247
  697.1 448.6 %reduce-scatter.20.cloned.1.call-start = ((), (), s32[]{:S(2)}) async-start(), calls=%async_computation.24 | async-start | bytes 14155776 | tf_op jit(solution)/shard_map/reduce_scatter | solution.py:250
  710.9 491.4 %all-gather.24.cloned.1.call-start = ((), (), s32[]{:S(2)}) async-start(), calls=%async_computation.25 | async-start | bytes 2949120 | tf_op jit(solution)/shard_map/all_gather | solution.py:309
  710.9 435.3 %copy-start.10 = (f32[512,1536]{1,0:T(8,128)S(1)}, f32[512,1536]{1,0:T(8,128)}, u32[]{:S(2)}) copy-start(f32[512,1536]{1,0:T(8,128)} %copy-done.8) | copy-start | bytes 9437188
  711.5 697.6 %all-reduce.10.cloned.1.call-start = ((), (), s32[]{:S(2)}) async-start(), calls=%async_computation.26 | async-start | bytes 11796480 | tf_op jit(solution)/shard_map/psum | solution.py:312
  1146.3 12.4 copy-start.20
  1158.7 4.7 copy-start.11
  1158.7 4.7 copy-start.17
  1166.3 3.7 copy-start.39
  1409.1 3.6 copy-start.29
  1414.7 3.2 copy-start.32
  1414.7 4.1 copy-start.31
  (18 other events, 33.4 us)
Sparse Core Ops, SparseCore 0:
  9.9 31.8 all-gather.11
  43.6 28.8 all-gather.13
  74.4 38.7 all-gather.9
  115.0 38.7 all-gather.15
  155.5 71.9 all-gather.17
  229.3 71.9 all-gather.19
  303.2 71.9 all-gather.21
  656.8 51.9 reduce-scatter.7
  712.3 53.7 reduce-scatter.13
  769.8 42.3 reduce-scatter.9
  816.1 42.3 reduce-scatter.11
  861.9 92.3 reduce-scatter.15
  957.7 92.2 reduce-scatter.17
  1053.4 92.2 reduce-scatter.19
  1147.1 50.2 all-gather.23
  1200.1 208.9 all-reduce.9
